TPU v7x, 128 devices: a whole 4x4x4 slice. The times are simulated.
128 devices in a mesh: ty: 8 (over x, core), tx: 16 (over y, z).
Axes of the slice: x: 4, y: 4, z: 4, core: 2. Of those that a mesh axis runs over, the one named last changes fastest.
Arguments:
- measured: float32 [8, 16, 32, 128, 128], P('ty', 'tx'), may hold values from 0 to 4
- positions: int32 [8, 16, 32, 2], P('ty', 'tx'), may hold values from 0 to 511, as said below
- owners: int32 [8, 16, 32], P('ty', 'tx'), may hold values from 0 to 127, as said below
- counts: int32 [8, 16], P('ty', 'tx'), may hold values from 16 to 32, as said below
- object_field: float32 [2, 4096, 8192], P(None, 'ty', 'tx'), may hold values from -4 to 4
- probe_field: float32 [2, 128, 128], replicated, may hold values from -6 to 6
Outputs:
- new_object: float32 [2, 4096, 8192], P(None, 'ty', 'tx')
- new_probe: float32 [2, 128, 128], replicated
Inputs may be any that keep to these rules, and one draw needn't show every extreme that they name: `positions`: for a live slot the entry is a cell of the owner's tile: row below 512, column below 512; other slots hold arbitrary cells of a tile. The owner of a live slot is the holding device's own tile or one of the up to eight tiles beside it (diagonals included). From one device at most 2 live slots go to any one other tile, and in every draw some tile receives exactly 2 from each of its eight neighbours. Slots that are not live hold arbitrary owners. `counts`: some device is full (32 live slots) in every draw.
All inputs are finite; a program needn't handle non-finite values.
Results may differ from a plain program's by a relative error of at most 0.0003.
Values sent between devices are 32-bit elements; how exact they have to be, the bound alone decides.
A program may use at most 128 MiB of HBM per device.

v0:
```python
import math
import jax
import jax.numpy as jnp
from jax import lax
from jax.sharding import PartitionSpec as P

M = 128
MOVE = 2
BLK = 8
offset_level = 1.0
floor_level = 1.0
tiny_level = 1e-06


def padded_2(value, sides, width):
    for axis, dim in sides:
        devices, length = (lax.axis_size(axis), value.shape[dim])
        up = [(i, (i + 1) % devices) for i in range(devices - 1)]
        down = [(j, i) for i, j in up]
        last = lax.slice_in_dim(value, length - width, length, axis=dim)
        leading = lax.slice_in_dim(value, 0, width, axis=dim)
        before = lax.ppermute(last, axis, up)
        after = lax.ppermute(leading, axis, down)
        value = jnp.concatenate([before, value, after], axis=dim)
    return value


def from_behind(block, axis, distance):
    devices = range(lax.axis_size(axis))
    route = [(i - distance, i) for i in devices if i - distance in devices]
    return lax.ppermute(block, axis, route)


def dft_tables(length_side):
    row_ids = lax.broadcasted_iota(jnp.int32, (length_side, length_side), 0)
    col_ids = lax.broadcasted_iota(jnp.int32, (length_side, length_side), 1)
    phase = (row_ids * col_ids % length_side).astype(jnp.float32) * (2.0 * math.pi / length_side)
    factor = 1.0 / math.sqrt(length_side)
    return (jnp.cos(phase) * factor, -jnp.sin(phase) * factor)


def transform(real_part, imag_part, cosine_table, sine_table):
    highest = lax.Precision.HIGHEST
    left_real = jnp.einsum("jk,bkl->bjl", cosine_table, real_part, precision=highest) - jnp.einsum(
        "jk,bkl->bjl", sine_table, imag_part, precision=highest
    )
    left_imag = jnp.einsum("jk,bkl->bjl", cosine_table, imag_part, precision=highest) + jnp.einsum(
        "jk,bkl->bjl", sine_table, real_part, precision=highest
    )
    outer_real = jnp.einsum("bjk,kl->bjl", left_real, cosine_table, precision=highest) - jnp.einsum(
        "bjk,kl->bjl", left_imag, sine_table, precision=highest
    )
    outer_imag = jnp.einsum("bjk,kl->bjl", left_real, sine_table, precision=highest) + jnp.einsum(
        "bjk,kl->bjl", left_imag, cosine_table, precision=highest
    )
    return (outer_real, outer_imag)


def pattern_terms(probe_field, patches, measured_block, live_mask, cosine_table, sine_table):
    probe_real = probe_field[0]
    probe_imag = probe_field[1]
    patch_real = patches[:, 0]
    patch_imag = patches[:, 1]
    exit_real = probe_real * patch_real - probe_imag * patch_imag
    exit_imag = probe_real * patch_imag + probe_imag * patch_real
    far_real, far_imag = transform(exit_real, exit_imag, cosine_table, sine_table)
    power = far_real * far_real + far_imag * far_imag
    ratio = 1.0 - measured_block / (power + offset_level)
    chi_real, chi_imag = transform(far_real * ratio, far_imag * ratio, cosine_table, -sine_table)
    chi_real = chi_real * live_mask[:, None, None]
    chi_imag = chi_imag * live_mask[:, None, None]
    object_real = probe_real * chi_real + probe_imag * chi_imag
    object_imag = probe_real * chi_imag - probe_imag * chi_real
    lighting = (probe_real * probe_real + probe_imag * probe_imag)[None] * live_mask[:, None, None]
    spread = jnp.stack([object_real, object_imag, lighting], axis=1)
    grad_real = jnp.sum(patch_real * chi_real + patch_imag * chi_imag, axis=0)
    grad_imag = jnp.sum(patch_real * chi_imag - patch_imag * chi_real, axis=0)
    weight = jnp.sum(
        (patch_real * patch_real + patch_imag * patch_imag) * live_mask[:, None, None], axis=0
    )
    return (spread, grad_real, grad_imag, weight)


def add_patches(accumulated, spread, start_rows, start_cols):
    zero_index = jnp.zeros((), jnp.int32)

    def add_one(patch_id, current):
        row_start = start_rows[patch_id]
        col_start = start_cols[patch_id]
        window = lax.dynamic_slice(current, (zero_index, row_start, col_start), spread.shape[1:])
        return lax.dynamic_update_slice(
            current, window + spread[patch_id], (zero_index, row_start, col_start)
        )

    return lax.fori_loop(0, spread.shape[0], add_one, accumulated)


def offsets(slot_tags, row_here, col_here, grid_cols):
    owner_id = slot_tags[:, 2] - 1
    is_valid = owner_id >= 0
    safe_owner = jnp.maximum(owner_id, 0)
    return (is_valid, safe_owner // grid_cols - row_here, safe_owner % grid_cols - col_here)


def select_slots(chosen, capacity, slot_rows, slot_tags):
    slot_count = chosen.shape[0]
    sort_key = jnp.where(chosen, 0, slot_count) + jnp.arange(slot_count, dtype=jnp.int32)
    picked = jnp.argsort(sort_key)[:capacity]
    kept_mask = jnp.take(chosen, picked)
    return (
        jnp.take(slot_rows, picked, axis=0),
        jnp.where(kept_mask[:, None], jnp.take(slot_tags, picked, axis=0), 0),
    )


def shards(measured, positions, owners, counts, object_field, probe_field):
    tile_rows = object_field.shape[1]
    tile_cols = object_field.shape[2]
    rim_width = M // 2
    grid_cols = lax.axis_size("tx")
    row_here = lax.axis_index("ty")
    col_here = lax.axis_index("tx")
    self_index = row_here * grid_cols + col_here
    padded = padded_2(object_field, (("ty", 1), ("tx", 2)), rim_width)
    own_rows = measured[0, 0]
    slot_ids = jnp.arange(own_rows.shape[0], dtype=jnp.int32)
    slot_alive = slot_ids < counts[0, 0]
    slot_info = jnp.concatenate([positions[0, 0], owners[0, 0][:, None]], axis=1) + 1
    own_tags = jnp.where(slot_alive[:, None], slot_info, 0)
    is_valid, row_offset, col_offset = offsets(own_tags, row_here, col_here, grid_cols)
    piece_rows = [own_rows]
    piece_tags = [own_tags]
    neighbours = [(-1, -1), (-1, 0), (-1, 1), (0, -1), (0, 1), (1, -1), (1, 0), (1, 1)]
    for down_step, right_step in neighbours:
        chosen = is_valid & (row_offset == down_step) & (col_offset == right_step)
        sent_rows, sent_tags = select_slots(chosen, MOVE, own_rows, own_tags)
        if down_step == 0:
            sent_rows, sent_tags = from_behind((sent_rows, sent_tags), "tx", right_step)
        elif right_step == 0:
            sent_rows, sent_tags = from_behind((sent_rows, sent_tags), "ty", down_step)
        else:
            sent_rows, sent_tags = from_behind((sent_rows, sent_tags), "tx", right_step)
            sent_rows, sent_tags = from_behind((sent_rows, sent_tags), "ty", down_step)
        piece_rows.append(sent_rows)
        piece_tags.append(sent_tags)
    all_rows = jnp.concatenate(piece_rows, axis=0)
    all_tags = jnp.concatenate(piece_tags, axis=0)
    valid_all = all_tags[:, 2] - 1 == self_index
    slot_total = all_rows.shape[0]
    slot_index = jnp.arange(slot_total, dtype=jnp.int32)
    slot_order = jnp.argsort(jnp.where(valid_all, 0, slot_total) + slot_index)
    block_turns = (jnp.sum(valid_all.astype(jnp.int32)) + BLK - 1) // BLK
    cosine_table, sine_table = dft_tables(M)
    zero_index = jnp.zeros((), jnp.int32)

    def one_block(block_id, state_carry):
        accumulated, grad_real, grad_imag, weight = state_carry
        picked = lax.dynamic_slice_in_dim(slot_order, block_id * BLK, BLK)
        block_rows = jnp.take(all_rows, picked, axis=0)
        block_tags = jnp.take(all_tags, picked, axis=0)
        live_mask = jnp.take(valid_all, picked).astype(jnp.float32)
        start_rows = jnp.clip(block_tags[:, 0] - 1, 0, tile_rows - 1)
        start_cols = jnp.clip(block_tags[:, 1] - 1, 0, tile_cols - 1)
        patches = jax.vmap(
            lambda row_start, col_start: lax.dynamic_slice(
                padded, (zero_index, row_start, col_start), (2, M, M)
            )
        )(start_rows, start_cols)
        spread, part_real, part_imag, part_weight = pattern_terms(
            probe_field, patches, block_rows, live_mask, cosine_table, sine_table
        )
        accumulated = add_patches(accumulated, spread, start_rows, start_cols)
        return (accumulated, grad_real + part_real, grad_imag + part_imag, weight + part_weight)

    start_state = (
        jnp.zeros((3, tile_rows + M, tile_cols + M), jnp.float32),
        jnp.zeros((M, M), jnp.float32),
        jnp.zeros((M, M), jnp.float32),
        jnp.zeros((M, M), jnp.float32),
    )
    accumulated, grad_real, grad_imag, weight = lax.fori_loop(
        0, block_turns, one_block, start_state
    )
    for direction in (1, -1):
        rim_strip = (
            accumulated[:, tile_rows + rim_width :, :]
            if direction == 1
            else accumulated[:, :rim_width, :]
        )
        arrived = from_behind(rim_strip, "ty", direction)
        if direction == 1:
            accumulated = accumulated.at[:, rim_width : 2 * rim_width, :].add(arrived)
        else:
            accumulated = accumulated.at[:, tile_rows : tile_rows + rim_width, :].add(arrived)
    for direction in (1, -1):
        rim_strip = (
            accumulated[:, :, tile_cols + rim_width :]
            if direction == 1
            else accumulated[:, :, :rim_width]
        )
        arrived = from_behind(rim_strip, "tx", direction)
        if direction == 1:
            accumulated = accumulated.at[:, :, rim_width : 2 * rim_width].add(arrived)
        else:
            accumulated = accumulated.at[:, :, tile_cols : tile_cols + rim_width].add(arrived)
    interior = accumulated[:, rim_width : rim_width + tile_rows, rim_width : rim_width + tile_cols]
    new_object = object_field - interior[:2] / (interior[2] + floor_level)
    summed = lax.psum((grad_real, grad_imag, weight), ("ty", "tx"))
    new_probe = probe_field - jnp.stack([summed[0], summed[1]]) / (summed[2] + tiny_level)
    return (new_object, new_probe)


def solution(mesh):
    placed = (
        P("ty", "tx", None, None, None),
        P("ty", "tx", None, None),
        P("ty", "tx", None),
        P("ty", "tx"),
        P(None, "ty", "tx"),
        P(),
    )
    return jax.shard_map(
        shards, mesh=mesh, in_specs=placed, out_specs=(P(None, "ty", "tx"), P()), check_vma=False
    )
```

profile of v0, /device:TPU:1, one launch (start us, length us, event | category | flops | bytes accessed | tf_op | source)
XLA Modules:
  0.0 1042.0 jit_solution(12287225430988321243)
XLA Ops:
  24.3 4.9 collective-permute-start.3
  69.9 4.3 collective-permute-start.10
  74.2 5.3 collective-permute-start.26
  79.6 5.7 collective-permute-start.19
  105.3 4.3 collective-permute-start.11
  117.8 4.2 collective-permute-start.25
  131.0 7.0 collective-permute-start.22
  155.1 5.0 collective-permute-done.15
  163.8 4.6 copy.126
  170.9 399.6 %while.52 = (s32[]{:T(128)}, f32[3,640,640]{2,1,0:T(8,128)}, f32[128,128]{1,0:T(8,128)S(1)}, f32[128,128]{1,0:T(8,128)S(1)}, f32[128,128]{1,0:T(8,128)S(1)}, /*i...) while((s32[]{:T(128)}, f32[3,640,640]{2,1,0:T(8,128)}, ...), condition=%wide.region_16.20_spmd.clone.clone, body=%wide.region_10.19_spmd.clone.clone.sunk | while | flops 3232875776 | bytes 34477920 | solution.py:181
  175.1 24.4 %while.53 = (s32[]{:T(128)}, f32[2,640,640]{2,1,0:T(8,128)}, s32[8,3]{1,0:T(8,128)S(1)}, f32[8,2,128,128]{3,2,0,1:T(8,128)S(1)}, s32[]{:T(128)}) while((s32[]{:T(128)}, f32[2,640,640]{2,1,0:T(8,128)}, s32[8,3]{1,0:T(8,128)S(1)}, f32[8,2,128,128]{3,2,0,1:T(8,128)S(1)}, s32[]{:T(128)}) %tuple.186), condition=%wide.while_cond.4, body=%wide.while_body.4.sunk | while | flops 2 | bytes 262269 | solution.py:165
  218.6 85.6 %while.54 = (s32[]{:T(128)}, f32[3,640,640]{2,1,0:T(8,128)}, s32[8]{0:T(128)S(1)}, s32[8]{0:T(128)S(1)}, f32[8,3,128,128]{3,2,0,1:T(8,128)S(1)}, /*index=5*/s32[]{:T(128)}, s32[]{:T(128)}, s32[]{:T(128)}) while((s32[]{:T(128)}, f32[3,640,640]{2,1,0:T(8,128)}, s32[8]{0:T(128)S(1)}, s32[8]{0:T(128)S(1)}, f32[8,3,128,128]{3,2,0,1:T(8,128)S(1)}, ...), condition=%wide.region_12.15_spmd, body=%wide.region_11.14_spmd.sunk | while | flops 49160 | bytes 983241 | solution.py:95
  257.4 4.1 dynamic_update_slice.8
  308.5 24.4 %while.53 = (s32[]{:T(128)}, f32[2,640,640]{2,1,0:T(8,128)}, s32[8,3]{1,0:T(8,128)S(1)}, f32[8,2,128,128]{3,2,0,1:T(8,128)S(1)}, s32[]{:T(128)}) while((s32[]{:T(128)}, f32[2,640,640]{2,1,0:T(8,128)}, s32[8,3]{1,0:T(8,128)S(1)}, f32[8,2,128,128]{3,2,0,1:T(8,128)S(1)}, s32[]{:T(128)}) %tuple.186), condition=%wide.while_cond.4, body=%wide.while_body.4.sunk | while | flops 2 | bytes 262269 | solution.py:165
  352.0 85.3 %while.54 = (s32[]{:T(128)}, f32[3,640,640]{2,1,0:T(8,128)}, s32[8]{0:T(128)S(1)}, s32[8]{0:T(128)S(1)}, f32[8,3,128,128]{3,2,0,1:T(8,128)S(1)}, /*index=5*/s32[]{:T(128)}, s32[]{:T(128)}, s32[]{:T(128)}) while((s32[]{:T(128)}, f32[3,640,640]{2,1,0:T(8,128)}, s32[8]{0:T(128)S(1)}, s32[8]{0:T(128)S(1)}, f32[8,3,128,128]{3,2,0,1:T(8,128)S(1)}, ...), condition=%wide.region_12.15_spmd, body=%wide.region_11.14_spmd.sunk | while | flops 49160 | bytes 983241 | solution.py:95
  358.7 4.1 dynamic_update_slice.8
  390.4 4.1 dynamic_update_slice.8
  401.2 4.1 dynamic_update_slice.8
  441.5 24.4 %while.53 = (s32[]{:T(128)}, f32[2,640,640]{2,1,0:T(8,128)}, s32[8,3]{1,0:T(8,128)S(1)}, f32[8,2,128,128]{3,2,0,1:T(8,128)S(1)}, s32[]{:T(128)}) while((s32[]{:T(128)}, f32[2,640,640]{2,1,0:T(8,128)}, s32[8,3]{1,0:T(8,128)S(1)}, f32[8,2,128,128]{3,2,0,1:T(8,128)S(1)}, s32[]{:T(128)}) %tuple.186), condition=%wide.while_cond.4, body=%wide.while_body.4.sunk | while | flops 2 | bytes 262269 | solution.py:165
  485.0 85.4 %while.54 = (s32[]{:T(128)}, f32[3,640,640]{2,1,0:T(8,128)}, s32[8]{0:T(128)S(1)}, s32[8]{0:T(128)S(1)}, f32[8,3,128,128]{3,2,0,1:T(8,128)S(1)}, /*index=5*/s32[]{:T(128)}, s32[]{:T(128)}, s32[]{:T(128)}) while((s32[]{:T(128)}, f32[3,640,640]{2,1,0:T(8,128)}, s32[8]{0:T(128)S(1)}, s32[8]{0:T(128)S(1)}, f32[8,3,128,128]{3,2,0,1:T(8,128)S(1)}, ...), condition=%wide.region_12.15_spmd, body=%wide.region_11.14_spmd.sunk | while | flops 49160 | bytes 983241 | solution.py:95
  491.7 4.1 dynamic_update_slice.8
  502.4 4.1 dynamic_update_slice.8
  534.3 4.1 dynamic_update_slice.8
  555.7 4.1 dynamic_update_slice.8
  571.6 4.3 collective-permute-start.28
  575.9 5.8 collective-permute-done.28
  586.5 135.1 %collective-permute-done.29 = f32[3,64,640]{2,1,0:T(8,128)S(1)} collective-permute-done((f32[3,64,640]{2,1,0:T(8,128)S(1)}, f32[3,64,640]{2,1,0:T(8,128)S(1)}, u32[]{:S(2)}, u32[]{:S(2)}) %collective-permute-start.29) | collective-permute-done | bytes 491552 | tf_op jit(solution)/shard_map/ppermute | solution.py:31
  725.4 13.1 %collective-permute-start.30 = (f32[3,640,64]{1,2,0:T(8,128)S(1)}, f32[3,640,64]{1,2,0:T(8,128)S(1)}, u32[]{:S(2)}, u32[]{:S(2)}) collective-permute-start(f32[3,640,64]{1,2,0:T(8,128)S(1)} %copy.127), channel_id=1, source_target_pairs={{0,1},{1,2},{2,3},{3,4},{4,5},{5,6},{6,7},{7,8},{8,9},{9,10},{10,1... | collective-permute-start | bytes 1474568 | tf_op jit(solution)/shard_map/ppermute | solution.py:31
  738.5 5.7 collective-permute-done.30
  746.1 9.2 scatter-add.16
  758.1 259.3 %all-reduce.3.cloned.1.call-done = (f32[1,128,128]{2,1,0:T(8,128)}, f32[1,128,128]{2,1,0:T(8,128)}, f32[128,128]{1,0:T(8,128)}) async-done(((f32[1,128,128]{2,1,0:T(8,128)}, f32[1,128,128]{2,1,0:T(8,128)}, f32[128,128]{1,0:T(8,128)}), (f32[1,128,128]{2,1,0:T(8,128)}, f32[1,128,128]{2,1,0:T(8,128)}, f32[128,128]{1,0:T(8,128)})) %all-reduce.3.cloned.1.call-update) | async-done | bytes 196624 | tf_op jit(solution)/shard_map/psum | solution.py:208
  1022.8 7.0 scatter-add.19
  (461 shorter events, 407.4 us)
Async XLA Ops:
  7.2 1010.2 %all-reduce.3.cloned.1.call-start = ((), (), s32[]{:S(2)}) async-start(), calls=%async_computation | async-start | bytes 393216 | tf_op jit(solution)/shard_map/psum | solution.py:208
  13.9 65.7 %collective-permute-start = (s32[2,3]{1,0:T(2,128)S(1)}, s32[2,3]{1,0:T(2,128)}, u32[]{:S(2)}, u32[]{:S(2)}) collective-permute-start(s32[2,3]{1,0:T(2,128)S(1)} %select_select_fusion.7), channel_id=1, source_target_pairs={{1,0},{2,1},{3,2},{4,3},{5,4},{6,5},{7,6},{8,7},{9,8},{10,9},{11,1... | collective-permute-start | bytes 80 | tf_op jit(solution)/shard_map/ppermute | solution.py:31
  16.5 48.0 %collective-permute-start.2 = (s32[2,3]{1,0:T(2,128)S(1)}, s32[2,3]{1,0:T(2,128)S(1)}, u32[]{:S(2)}, u32[]{:S(2)}) collective-permute-start(s32[2,3]{1,0:T(2,128)S(1)} %select_select_fusion.6), channel_id=1, source_target_pairs={{16,0},{32,16},{48,32},{64,48},{80,64},{96,80},{112,96},{17,1},{33... | collective-permute-start | bytes 80 | tf_op jit(solution)/shard_map/ppermute | solution.py:31
  24.3 61.1 %collective-permute-start.3 = (s32[2,3]{1,0:T(2,128)S(1)}, s32[2,3]{1,0:T(2,128)}, u32[]{:S(2)}, u32[]{:S(2)}) collective-permute-start(s32[2,3]{1,0:T(2,128)S(1)} %select_select_fusion.5), channel_id=1, source_target_pairs={{0,1},{1,2},{2,3},{3,4},{4,5},{5,6},{6,7},{7,8},{8,9},{9,10},{10,1... | collective-permute-start | bytes 80 | tf_op jit(solution)/shard_map/ppermute | solution.py:31
  30.4 35.4 %collective-permute-start.5 = (s32[2,3]{1,0:T(2,128)S(1)}, s32[2,3]{1,0:T(2,128)S(1)}, u32[]{:S(2)}, u32[]{:S(2)}) collective-permute-start(s32[2,3]{1,0:T(2,128)S(1)} %select_select_fusion.4), channel_id=1, source_target_pairs={{1,0},{2,1},{3,2},{4,3},{5,4},{6,5},{7,6},{8,7},{9,8},{10,9},{11,1... | collective-permute-start | bytes 80 | tf_op jit(solution)/shard_map/ppermute | solution.py:31
  36.8 33.0 %collective-permute-start.6 = (s32[2,3]{1,0:T(2,128)}, s32[2,3]{1,0:T(2,128)S(1)}, u32[]{:S(2)}, u32[]{:S(2)}) collective-permute-start(s32[2,3]{1,0:T(2,128)} %select_select_fusion.3), channel_id=1, source_target_pairs={{0,1},{1,2},{2,3},{3,4},{4,5},{5,6},{6,7},{7,8},{8,9},{9,10},{10,1... | collective-permute-start | bytes 80 | tf_op jit(solution)/shard_map/ppermute | solution.py:31
  64.4 32.5 %collective-permute-start.7 = (s32[2,3]{1,0:T(2,128)S(1)}, s32[2,3]{1,0:T(2,128)S(1)}, u32[]{:S(2)}, u32[]{:S(2)}) collective-permute-start(s32[2,3]{1,0:T(2,128)S(1)} %select_select_fusion.2), channel_id=1, source_target_pairs={{1,0},{2,1},{3,2},{4,3},{5,4},{6,5},{7,6},{8,7},{9,8},{10,9},{11,1... | collective-permute-start | bytes 80 | tf_op jit(solution)/shard_map/ppermute | solution.py:31
  65.8 8.4 collective-permute-start.9
  69.9 29.0 %collective-permute-start.10 = (s32[2,3]{1,0:T(2,128)S(1)}, s32[2,3]{1,0:T(2,128)S(1)}, u32[]{:S(2)}, u32[]{:S(2)}) collective-permute-start(s32[2,3]{1,0:T(2,128)S(1)} %select_select_fusion), channel_id=1, source_target_pairs={{0,1},{1,2},{2,3},{3,4},{4,5},{5,6},{6,7},{7,8},{8,9},{9,10},{10,1... | collective-permute-start | bytes 80 | tf_op jit(solution)/shard_map/ppermute | solution.py:31
  74.2 56.7 %collective-permute-start.26 = (f32[2,128,128]{2,1,0:T(8,128)}, f32[2,128,128]{2,1,0:T(8,128)}, u32[]{:S(2)}, u32[]{:S(2)}) collective-permute-start(f32[2,128,128]{2,1,0:T(8,128)} %broadcast_select_fusion.1), channel_id=1, source_target_pairs={{0,1},{1,2},{2,3},{3,4},{4,5},{5,6},{6,7},{7,8},{8,9},{9,10},{10,1... | collective-permute-start | bytes 393224 | tf_op jit(solution)/shard_map/ppermute | solution.py:31
  79.6 45.5 %collective-permute-start.19 = (f32[2,128,128]{2,1,0:T(8,128)}, f32[2,128,128]{2,1,0:T(8,128)}, u32[]{:S(2)}, u32[]{:S(2)}) collective-permute-start(f32[2,128,128]{2,1,0:T(8,128)} %broadcast_select_fusion.6), channel_id=1, source_target_pairs={{0,1},{1,2},{2,3},{3,4},{4,5},{5,6},{6,7},{7,8},{8,9},{9,10},{10,1... | collective-permute-start | bytes 393224 | tf_op jit(solution)/shard_map/ppermute | solution.py:31
  85.3 5.1 collective-permute-start.1
  90.4 5.1 collective-permute-start.4
  95.5 16.9 %collective-permute-start.16 = (f32[2,128,128]{2,1,0:T(8,128)}, f32[2,128,128]{2,1,0:T(8,128)}, u32[]{:S(2)}, u32[]{:S(2)}) collective-permute-start(f32[2,128,128]{2,1,0:T(8,128)} %broadcast_select_fusion.8), channel_id=1, source_target_pairs={{1,0},{2,1},{3,2},{4,3},{5,4},{6,5},{7,6},{8,7},{9,8},{10,9},{11,1... | collective-permute-start | bytes 393224 | tf_op jit(solution)/shard_map/ppermute | solution.py:31
  96.9 20.9 %collective-permute-start.12 = (f32[2,64,512]{1,2,0:T(8,128)}, f32[2,64,512]{1,2,0:T(8,128)S(1)}, u32[]{:S(2)}, u32[]{:S(2)}) collective-permute-start(f32[2,64,512]{1,2,0:T(8,128)} %get-tuple-element.723), channel_id=1, source_target_pairs={{0,16},{16,32},{32,48},{48,64},{64,80},{80,96},{96,112},{1,17},{17... | collective-permute-start | bytes 786440 | tf_op jit(solution)/shard_map/ppermute | solution.py:22
  98.9 6.4 collective-permute-start.8
  110.3 11.7 %collective-permute-start.13 = (f32[2,64,512]{1,2,0:T(8,128)}, f32[2,64,512]{1,2,0:T(8,128)}, u32[]{:S(2)}, u32[]{:S(2)}) collective-permute-start(f32[2,64,512]{1,2,0:T(8,128)} %get-tuple-element.724), channel_id=1, source_target_pairs={{16,0},{32,16},{48,32},{64,48},{80,64},{96,80},{112,96},{17,1},{33... | collective-permute-start | bytes 786440 | tf_op jit(solution)/shard_map/ppermute | solution.py:23
  112.4 14.0 %collective-permute-start.17 = (f32[2,128,128]{2,1,0:T(8,128)}, f32[2,128,128]{2,1,0:T(8,128)S(1)}, u32[]{:S(2)}, u32[]{:S(2)}) collective-permute-start(f32[2,128,128]{2,1,0:T(8,128)} %collective-permute-done.16), channel_id=1, source_target_pairs={{16,0},{32,16},{48,32},{64,48},{80,64},{96,80},{112,96},{17,1},{33... | collective-permute-start | bytes 393224 | tf_op jit(solution)/shard_map/ppermute | solution.py:31
  117.8 33.8 %collective-permute-start.25 = (f32[2,128,128]{2,1,0:T(8,128)S(1)}, f32[2,128,128]{2,1,0:T(8,128)S(1)}, u32[]{:S(2)}, u32[]{:S(2)}) collective-permute-start(f32[2,128,128]{2,1,0:T(8,128)S(1)} %broadcast_select_fusion.2), channel_id=1, source_target_pairs={{0,16},{16,32},{32,48},{48,64},{64,80},{80,96},{96,112},{1,17},{17... | collective-permute-start | bytes 393224 | tf_op jit(solution)/shard_map/ppermute | solution.py:31
  122.0 7.0 collective-permute-start.18
  125.1 12.9 %collective-permute-start.23 = (f32[2,128,128]{2,1,0:T(8,128)S(1)}, f32[2,128,128]{2,1,0:T(8,128)S(1)}, u32[]{:S(2)}, u32[]{:S(2)}) collective-permute-start(f32[2,128,128]{2,1,0:T(8,128)S(1)} %broadcast_select_fusion.3), channel_id=1, source_target_pairs={{1,0},{2,1},{3,2},{4,3},{5,4},{6,5},{7,6},{8,7},{9,8},{10,9},{11,1... | collective-permute-start | bytes 393224 | tf_op jit(solution)/shard_map/ppermute | solution.py:31
  126.4 15.5 %collective-permute-start.20 = (f32[2,128,128]{2,1,0:T(8,128)}, f32[2,128,128]{2,1,0:T(8,128)S(1)}, u32[]{:S(2)}, u32[]{:S(2)}) collective-permute-start(f32[2,128,128]{2,1,0:T(8,128)} %collective-permute-done.19), channel_id=1, source_target_pairs={{16,0},{32,16},{48,32},{64,48},{80,64},{96,80},{112,96},{17,1},{33... | collective-permute-start | bytes 393224 | tf_op jit(solution)/shard_map/ppermute | solution.py:31
  129.0 15.7 %collective-permute-start.21 = (f32[2,128,128]{2,1,0:T(8,128)}, f32[2,128,128]{2,1,0:T(8,128)S(1)}, u32[]{:S(2)}, u32[]{:S(2)}) collective-permute-start(f32[2,128,128]{2,1,0:T(8,128)} %broadcast_select_fusion.5), channel_id=1, source_target_pairs={{1,0},{2,1},{3,2},{4,3},{5,4},{6,5},{7,6},{8,7},{9,8},{10,9},{11,1... | collective-permute-start | bytes 393224 | tf_op jit(solution)/shard_map/ppermute | solution.py:31
  131.0 18.1 %collective-permute-start.22 = (f32[2,128,128]{2,1,0:T(8,128)}, f32[2,128,128]{2,1,0:T(8,128)S(1)}, u32[]{:S(2)}, u32[]{:S(2)}) collective-permute-start(f32[2,128,128]{2,1,0:T(8,128)} %broadcast_select_fusion.4), channel_id=1, source_target_pairs={{0,1},{1,2},{2,3},{3,4},{4,5},{5,6},{6,7},{7,8},{8,9},{9,10},{10,1... | collective-permute-start | bytes 393224 | tf_op jit(solution)/shard_map/ppermute | solution.py:31
  138.0 14.3 %collective-permute-start.27 = (f32[2,128,128]{2,1,0:T(8,128)}, f32[2,128,128]{2,1,0:T(8,128)S(1)}, u32[]{:S(2)}, u32[]{:S(2)}) collective-permute-start(f32[2,128,128]{2,1,0:T(8,128)} %collective-permute-done.26), channel_id=1, source_target_pairs={{0,16},{16,32},{32,48},{48,64},{64,80},{80,96},{96,112},{1,17},{17... | collective-permute-start | bytes 393224 | tf_op jit(solution)/shard_map/ppermute | solution.py:31
  141.9 9.1 collective-permute-start.24
  144.7 10.4 collective-permute-start.14
  149.0 11.1 %collective-permute-start.15 = (f32[2,640,64]{1,2,0:T(8,128)S(1)}, f32[2,640,64]{1,2,0:T(8,128)S(1)}, u32[]{:S(2)}, u32[]{:S(2)}) collective-permute-start(f32[2,640,64]{1,2,0:T(8,128)S(1)} %get-tuple-element.722), channel_id=1, source_target_pairs={{1,0},{2,1},{3,2},{4,3},{5,4},{6,5},{7,6},{8,7},{9,8},{10,9},{11,1... | collective-permute-start | bytes 983048 | tf_op jit(solution)/shard_map/ppermute | solution.py:23
  571.6 10.0 collective-permute-start.28
  584.6 137.0 %collective-permute-start.29 = (f32[3,64,640]{2,1,0:T(8,128)S(1)}, f32[3,64,640]{2,1,0:T(8,128)S(1)}, u32[]{:S(2)}, u32[]{:S(2)}) collective-permute-start(f32[3,64,640]{2,1,0:T(8,128)S(1)} %slice.318), channel_id=1, source_target_pairs={{16,0},{32,16},{48,32},{64,48},{80,64},{96,80},{112,96},{17,1},{33... | collective-permute-start | bytes 1474568 | tf_op jit(solution)/shard_map/ppermute | solution.py:31
  725.4 18.8 %collective-permute-start.30 = (f32[3,640,64]{1,2,0:T(8,128)S(1)}, f32[3,640,64]{1,2,0:T(8,128)S(1)}, u32[]{:S(2)}, u32[]{:S(2)}) collective-permute-start(f32[3,640,64]{1,2,0:T(8,128)S(1)} %copy.127), channel_id=1, source_target_pairs={{0,1},{1,2},{2,3},{3,4},{4,5},{5,6},{6,7},{7,8},{8,9},{9,10},{10,1... | collective-permute-start | bytes 1474568 | tf_op jit(solution)/shard_map/ppermute | solution.py:31
  756.8 263.0 %collective-permute-start.31 = (f32[3,640,64]{1,2,0:T(8,128)S(1)}, f32[3,640,64]{1,2,0:T(8,128)S(1)}, u32[]{:S(2)}, u32[]{:S(2)}) collective-permute-start(f32[3,640,64]{1,2,0:T(8,128)S(1)} %copy.129), channel_id=1, source_target_pairs={{1,0},{2,1},{3,2},{4,3},{5,4},{6,5},{7,6},{8,7},{9,8},{10,9},{11,1... | collective-permute-start | bytes 1474568 | tf_op jit(solution)/shard_map/ppermute | solution.py:31
  (9 other events, 529.5 us)
Sparse Core Ops, SparseCore 0:
  738.6 278.7 all-reduce.2
where the time goes:
time: 1050 us; the launch traced here: 1040 us
  waiting for transfers between devices  423 us (40%)
  local copies, waits for them, and re-layouts  269 us (26%)
  starting transfers between devices  103 us (10%)
  loops' own time  101 us (10%)
  other arithmetic  73.1 us (7%)
  matrix products  56.2 us (5%)
  between operations  16.2 us (2%)
    psum x1, waiting for transfers between devices, shards(): summed = lax.psum((grad_real, grad_imag, weight), ('ty', 'tx'))  259 us
    ppermute x28, waiting for transfers between devices, from_behind(): return lax.ppermute(block, axis, route)  156 us
    another operation x3, loops' own time, add_patches(): return lax.fori_loop(0, spread.shape[0], add_one, accumulated)  100 us
    dynamic_update_slice x24, local copies, waits for them, and re-layouts, add_one(): lax.dynamic_update_slice(current, window + spread[patch_id], (zero_index,...  96.4 us
    ppermute x28, starting transfers between devices, from_behind(): return lax.ppermute(block, axis, route)  94.2 us
    gather x72, local copies, waits for them, and re-layouts  72.6 us
    add x24, other arithmetic, add_one(): window + spread[patch_id]  27.6 us
  transfers between devices with their start and end apart: 33, of which 10 were waited for; matrix products, arithmetic and copies ran while one was open for 6% of the time, Pallas kernels for 0%

commit v1 on v0

--- a/solution.py
+++ b/solution.py
@@ -205,7 +205,7 @@
             accumulated = accumulated.at[:, :, tile_cols : tile_cols + rim_width].add(arrived)
     interior = accumulated[:, rim_width : rim_width + tile_rows, rim_width : rim_width + tile_cols]
     new_object = object_field - interior[:2] / (interior[2] + floor_level)
-    summed = lax.psum((grad_real, grad_imag, weight), ("ty", "tx"))
+    summed = lax.psum(lax.psum((grad_real, grad_imag, weight), "ty"), "tx")
     new_probe = probe_field - jnp.stack([summed[0], summed[1]]) / (summed[2] + tiny_level)
     return (new_object, new_probe)
 

time: 1050 us -> 1060 us (level)
    psum x1 -> x2, waiting for transfers between devices: 259 us -> 271 us  [shards(): summed = lax.psum(lax.psum((grad_real, grad_imag, weight), 'ty'), 'tx')]
  transfers between devices with their start and end apart: 33 -> 34, of which waited for: 10 -> 10; matrix products, arithmetic and copies ran while one was open for 6% -> 6% of each run, Pallas kernels for 0% -> 0%
where the time goes in v1:
time: 1060 us; the launch traced here: 1050 us
  waiting for transfers between devices  429 us (40%)
  local copies, waits for them, and re-layouts  269 us (25%)
  starting transfers between devices  103 us (10%)
  loops' own time  101 us (10%)
  other arithmetic  73.1 us (7%)
  matrix products  56.2 us (5%)
  between operations  16.2 us (2%)
    psum x2, waiting for transfers between devices, shards(): summed = lax.psum(lax.psum((grad_real, grad_imag, weight), 'ty'), 'tx')  271 us
    ppermute x28, waiting for transfers between devices, from_behind(): return lax.ppermute(block, axis, route)  151 us
    another operation x3, loops' own time, add_patches(): return lax.fori_loop(0, spread.shape[0], add_one, accumulated)  100 us
    dynamic_update_slice x24, local copies, waits for them, and re-layouts, add_one(): lax.dynamic_update_slice(current, window + spread[patch_id], (zero_index,...  96.4 us
    ppermute x28, starting transfers between devices, from_behind(): return lax.ppermute(block, axis, route)  94.2 us
    gather x72, local copies, waits for them, and re-layouts  72.6 us
    add x24, other arithmetic, add_one(): window + spread[patch_id]  27.6 us
  transfers between devices with their start and end apart: 34, of which 10 were waited for; matrix products, arithmetic and copies ran while one was open for 6% of the time, Pallas kernels for 0%

profile of v1, /device:TPU:1, one launch (start us, length us, event | category | flops | bytes accessed | tf_op | source)
XLA Modules:
  0.0 1048.2 jit_solution(14792590855650351858)
XLA Ops:
  24.3 4.9 collective-permute-start.3
  69.9 4.3 collective-permute-start.10
  74.2 5.3 collective-permute-start.26
  79.6 5.7 collective-permute-start.19
  105.3 4.3 collective-permute-start.11
  117.8 4.2 collective-permute-start.25
  131.0 7.0 collective-permute-start.22
  155.1 5.0 collective-permute-done.15
  163.8 4.6 copy.126
  170.9 399.6 %while.52 = (s32[]{:T(128)}, f32[3,640,640]{2,1,0:T(8,128)}, f32[128,128]{1,0:T(8,128)S(1)}, f32[128,128]{1,0:T(8,128)S(1)}, f32[128,128]{1,0:T(8,128)S(1)}, /*i...) while((s32[]{:T(128)}, f32[3,640,640]{2,1,0:T(8,128)}, ...), condition=%wide.region_16.20_spmd.clone.clone, body=%wide.region_10.19_spmd.clone.clone.sunk | while | flops 3232875776 | bytes 34477920 | solution.py:181
  175.1 24.4 %while.53 = (s32[]{:T(128)}, f32[2,640,640]{2,1,0:T(8,128)}, s32[8,3]{1,0:T(8,128)S(1)}, f32[8,2,128,128]{3,2,0,1:T(8,128)S(1)}, s32[]{:T(128)}) while((s32[]{:T(128)}, f32[2,640,640]{2,1,0:T(8,128)}, s32[8,3]{1,0:T(8,128)S(1)}, f32[8,2,128,128]{3,2,0,1:T(8,128)S(1)}, s32[]{:T(128)}) %tuple.186), condition=%wide.while_cond.4, body=%wide.while_body.4.sunk | while | flops 2 | bytes 262269 | solution.py:165
  218.6 85.6 %while.54 = (s32[]{:T(128)}, f32[3,640,640]{2,1,0:T(8,128)}, s32[8]{0:T(128)S(1)}, s32[8]{0:T(128)S(1)}, f32[8,3,128,128]{3,2,0,1:T(8,128)S(1)}, /*index=5*/s32[]{:T(128)}, s32[]{:T(128)}, s32[]{:T(128)}) while((s32[]{:T(128)}, f32[3,640,640]{2,1,0:T(8,128)}, s32[8]{0:T(128)S(1)}, s32[8]{0:T(128)S(1)}, f32[8,3,128,128]{3,2,0,1:T(8,128)S(1)}, ...), condition=%wide.region_12.15_spmd, body=%wide.region_11.14_spmd.sunk | while | flops 49160 | bytes 983241 | solution.py:95
  257.4 4.1 dynamic_update_slice.8
  308.5 24.4 %while.53 = (s32[]{:T(128)}, f32[2,640,640]{2,1,0:T(8,128)}, s32[8,3]{1,0:T(8,128)S(1)}, f32[8,2,128,128]{3,2,0,1:T(8,128)S(1)}, s32[]{:T(128)}) while((s32[]{:T(128)}, f32[2,640,640]{2,1,0:T(8,128)}, s32[8,3]{1,0:T(8,128)S(1)}, f32[8,2,128,128]{3,2,0,1:T(8,128)S(1)}, s32[]{:T(128)}) %tuple.186), condition=%wide.while_cond.4, body=%wide.while_body.4.sunk | while | flops 2 | bytes 262269 | solution.py:165
  352.0 85.3 %while.54 = (s32[]{:T(128)}, f32[3,640,640]{2,1,0:T(8,128)}, s32[8]{0:T(128)S(1)}, s32[8]{0:T(128)S(1)}, f32[8,3,128,128]{3,2,0,1:T(8,128)S(1)}, /*index=5*/s32[]{:T(128)}, s32[]{:T(128)}, s32[]{:T(128)}) while((s32[]{:T(128)}, f32[3,640,640]{2,1,0:T(8,128)}, s32[8]{0:T(128)S(1)}, s32[8]{0:T(128)S(1)}, f32[8,3,128,128]{3,2,0,1:T(8,128)S(1)}, ...), condition=%wide.region_12.15_spmd, body=%wide.region_11.14_spmd.sunk | while | flops 49160 | bytes 983241 | solution.py:95
  358.7 4.1 dynamic_update_slice.8
  390.4 4.1 dynamic_update_slice.8
  401.2 4.1 dynamic_update_slice.8
  441.5 24.4 %while.53 = (s32[]{:T(128)}, f32[2,640,640]{2,1,0:T(8,128)}, s32[8,3]{1,0:T(8,128)S(1)}, f32[8,2,128,128]{3,2,0,1:T(8,128)S(1)}, s32[]{:T(128)}) while((s32[]{:T(128)}, f32[2,640,640]{2,1,0:T(8,128)}, s32[8,3]{1,0:T(8,128)S(1)}, f32[8,2,128,128]{3,2,0,1:T(8,128)S(1)}, s32[]{:T(128)}) %tuple.186), condition=%wide.while_cond.4, body=%wide.while_body.4.sunk | while | flops 2 | bytes 262269 | solution.py:165
  485.0 85.4 %while.54 = (s32[]{:T(128)}, f32[3,640,640]{2,1,0:T(8,128)}, s32[8]{0:T(128)S(1)}, s32[8]{0:T(128)S(1)}, f32[8,3,128,128]{3,2,0,1:T(8,128)S(1)}, /*index=5*/s32[]{:T(128)}, s32[]{:T(128)}, s32[]{:T(128)}) while((s32[]{:T(128)}, f32[3,640,640]{2,1,0:T(8,128)}, s32[8]{0:T(128)S(1)}, s32[8]{0:T(128)S(1)}, f32[8,3,128,128]{3,2,0,1:T(8,128)S(1)}, ...), condition=%wide.region_12.15_spmd, body=%wide.region_11.14_spmd.sunk | while | flops 49160 | bytes 983241 | solution.py:95
  491.7 4.1 dynamic_update_slice.8
  502.4 4.1 dynamic_update_slice.8
  534.3 4.1 dynamic_update_slice.8
  555.7 4.1 dynamic_update_slice.8
  571.6 4.3 collective-permute-start.28
  575.9 5.8 collective-permute-done.28
  586.5 135.1 %collective-permute-done.29 = f32[3,64,640]{2,1,0:T(8,128)S(1)} collective-permute-done((f32[3,64,640]{2,1,0:T(8,128)S(1)}, f32[3,64,640]{2,1,0:T(8,128)S(1)}, u32[]{:S(2)}, u32[]{:S(2)}) %collective-permute-start.29) | collective-permute-done | bytes 491552 | tf_op jit(solution)/shard_map/ppermute | solution.py:31
  725.4 13.1 %collective-permute-start.30 = (f32[3,640,64]{1,2,0:T(8,128)S(1)}, f32[3,640,64]{1,2,0:T(8,128)S(1)}, u32[]{:S(2)}, u32[]{:S(2)}) collective-permute-start(f32[3,640,64]{1,2,0:T(8,128)S(1)} %copy.127), channel_id=1, source_target_pairs={{0,1},{1,2},{2,3},{3,4},{4,5},{5,6},{6,7},{7,8},{8,9},{9,10},{10,1... | collective-permute-start | bytes 1474568 | tf_op jit(solution)/shard_map/ppermute | solution.py:31
  738.5 191.2 %all-reduce.7.cloned.1.call-done = (f32[128,128]{1,0:T(8,128)}, f32[128,128]{1,0:T(8,128)}, f32[128,128]{1,0:T(8,128)}) async-done(((f32[128,128]{1,0:T(8,128)}, f32[128,128]{1,0:T(8,128)}, f32[128,128]{1,0:T(8,128)}), (f32[128,128]{1,0:T(8,128)}, f32[128,128]{1,0:T(8,128)}, f32[128,128]{1,0:T(8,128)})) %all-reduce.7.cloned.1.call-update) | async-done | bytes 196624 | tf_op jit(solution)/shard_map/psum | solution.py:208
  931.7 9.2 scatter-add.16
  943.8 79.9 %all-reduce.5.cloned.1.call-done = (f32[1,128,128]{2,1,0:T(8,128)}, f32[1,128,128]{2,1,0:T(8,128)}, f32[128,128]{1,0:T(8,128)}) async-done(((f32[1,128,128]{2,1,0:T(8,128)}, f32[1,128,128]{2,1,0:T(8,128)}, f32[128,128]{1,0:T(8,128)}), (f32[1,128,128]{2,1,0:T(8,128)}, f32[1,128,128]{2,1,0:T(8,128)}, f32[128,128]{1,0:T(8,128)})) %all-reduce.5.cloned.1.call-update) | async-done | bytes 196624 | tf_op jit(solution)/shard_map/psum | solution.py:208
  1029.1 7.0 scatter-add.19
  (464 shorter events, 407.4 us)
Async XLA Ops:
  7.2 922.6 %all-reduce.7.cloned.1.call-start = ((), (), s32[]{:S(2)}) async-start(), calls=%async_computation.1 | async-start | bytes 393216 | tf_op jit(solution)/shard_map/psum | solution.py:208
  13.9 65.7 %collective-permute-start = (s32[2,3]{1,0:T(2,128)S(1)}, s32[2,3]{1,0:T(2,128)}, u32[]{:S(2)}, u32[]{:S(2)}) collective-permute-start(s32[2,3]{1,0:T(2,128)S(1)} %select_select_fusion.7), channel_id=1, source_target_pairs={{1,0},{2,1},{3,2},{4,3},{5,4},{6,5},{7,6},{8,7},{9,8},{10,9},{11,1... | collective-permute-start | bytes 80 | tf_op jit(solution)/shard_map/ppermute | solution.py:31
  16.5 48.0 %collective-permute-start.2 = (s32[2,3]{1,0:T(2,128)S(1)}, s32[2,3]{1,0:T(2,128)S(1)}, u32[]{:S(2)}, u32[]{:S(2)}) collective-permute-start(s32[2,3]{1,0:T(2,128)S(1)} %select_select_fusion.6), channel_id=1, source_target_pairs={{16,0},{32,16},{48,32},{64,48},{80,64},{96,80},{112,96},{17,1},{33... | collective-permute-start | bytes 80 | tf_op jit(solution)/shard_map/ppermute | solution.py:31
  24.3 61.1 %collective-permute-start.3 = (s32[2,3]{1,0:T(2,128)S(1)}, s32[2,3]{1,0:T(2,128)}, u32[]{:S(2)}, u32[]{:S(2)}) collective-permute-start(s32[2,3]{1,0:T(2,128)S(1)} %select_select_fusion.5), channel_id=1, source_target_pairs={{0,1},{1,2},{2,3},{3,4},{4,5},{5,6},{6,7},{7,8},{8,9},{9,10},{10,1... | collective-permute-start | bytes 80 | tf_op jit(solution)/shard_map/ppermute | solution.py:31
  30.4 35.4 %collective-permute-start.5 = (s32[2,3]{1,0:T(2,128)S(1)}, s32[2,3]{1,0:T(2,128)S(1)}, u32[]{:S(2)}, u32[]{:S(2)}) collective-permute-start(s32[2,3]{1,0:T(2,128)S(1)} %select_select_fusion.4), channel_id=1, source_target_pairs={{1,0},{2,1},{3,2},{4,3},{5,4},{6,5},{7,6},{8,7},{9,8},{10,9},{11,1... | collective-permute-start | bytes 80 | tf_op jit(solution)/shard_map/ppermute | solution.py:31
  36.8 33.0 %collective-permute-start.6 = (s32[2,3]{1,0:T(2,128)}, s32[2,3]{1,0:T(2,128)S(1)}, u32[]{:S(2)}, u32[]{:S(2)}) collective-permute-start(s32[2,3]{1,0:T(2,128)} %select_select_fusion.3), channel_id=1, source_target_pairs={{0,1},{1,2},{2,3},{3,4},{4,5},{5,6},{6,7},{7,8},{8,9},{9,10},{10,1... | collective-permute-start | bytes 80 | tf_op jit(solution)/shard_map/ppermute | solution.py:31
  64.4 32.5 %collective-permute-start.7 = (s32[2,3]{1,0:T(2,128)S(1)}, s32[2,3]{1,0:T(2,128)S(1)}, u32[]{:S(2)}, u32[]{:S(2)}) collective-permute-start(s32[2,3]{1,0:T(2,128)S(1)} %select_select_fusion.2), channel_id=1, source_target_pairs={{1,0},{2,1},{3,2},{4,3},{5,4},{6,5},{7,6},{8,7},{9,8},{10,9},{11,1... | collective-permute-start | bytes 80 | tf_op jit(solution)/shard_map/ppermute | solution.py:31
  65.8 8.4 collective-permute-start.9
  69.9 29.0 %collective-permute-start.10 = (s32[2,3]{1,0:T(2,128)S(1)}, s32[2,3]{1,0:T(2,128)S(1)}, u32[]{:S(2)}, u32[]{:S(2)}) collective-permute-start(s32[2,3]{1,0:T(2,128)S(1)} %select_select_fusion), channel_id=1, source_target_pairs={{0,1},{1,2},{2,3},{3,4},{4,5},{5,6},{6,7},{7,8},{8,9},{9,10},{10,1... | collective-permute-start | bytes 80 | tf_op jit(solution)/shard_map/ppermute | solution.py:31
  74.2 56.7 %collective-permute-start.26 = (f32[2,128,128]{2,1,0:T(8,128)}, f32[2,128,128]{2,1,0:T(8,128)}, u32[]{:S(2)}, u32[]{:S(2)}) collective-permute-start(f32[2,128,128]{2,1,0:T(8,128)} %broadcast_select_fusion.1), channel_id=1, source_target_pairs={{0,1},{1,2},{2,3},{3,4},{4,5},{5,6},{6,7},{7,8},{8,9},{9,10},{10,1... | collective-permute-start | bytes 393224 | tf_op jit(solution)/shard_map/ppermute | solution.py:31
  79.6 45.5 %collective-permute-start.19 = (f32[2,128,128]{2,1,0:T(8,128)}, f32[2,128,128]{2,1,0:T(8,128)}, u32[]{:S(2)}, u32[]{:S(2)}) collective-permute-start(f32[2,128,128]{2,1,0:T(8,128)} %broadcast_select_fusion.6), channel_id=1, source_target_pairs={{0,1},{1,2},{2,3},{3,4},{4,5},{5,6},{6,7},{7,8},{8,9},{9,10},{10,1... | collective-permute-start | bytes 393224 | tf_op jit(solution)/shard_map/ppermute | solution.py:31
  85.3 5.1 collective-permute-start.1
  95.5 16.9 %collective-permute-start.16 = (f32[2,128,128]{2,1,0:T(8,128)}, f32[2,128,128]{2,1,0:T(8,128)}, u32[]{:S(2)}, u32[]{:S(2)}) collective-permute-start(f32[2,128,128]{2,1,0:T(8,128)} %broadcast_select_fusion.8), channel_id=1, source_target_pairs={{1,0},{2,1},{3,2},{4,3},{5,4},{6,5},{7,6},{8,7},{9,8},{10,9},{11,1... | collective-permute-start | bytes 393224 | tf_op jit(solution)/shard_map/ppermute | solution.py:31
  96.9 20.9 %collective-permute-start.12 = (f32[2,64,512]{1,2,0:T(8,128)}, f32[2,64,512]{1,2,0:T(8,128)S(1)}, u32[]{:S(2)}, u32[]{:S(2)}) collective-permute-start(f32[2,64,512]{1,2,0:T(8,128)} %get-tuple-element.726), channel_id=1, source_target_pairs={{0,16},{16,32},{32,48},{48,64},{64,80},{80,96},{96,112},{1,17},{17... | collective-permute-start | bytes 786440 | tf_op jit(solution)/shard_map/ppermute | solution.py:22
  98.9 6.4 collective-permute-start.8
  110.3 11.7 %collective-permute-start.13 = (f32[2,64,512]{1,2,0:T(8,128)}, f32[2,64,512]{1,2,0:T(8,128)}, u32[]{:S(2)}, u32[]{:S(2)}) collective-permute-start(f32[2,64,512]{1,2,0:T(8,128)} %get-tuple-element.727), channel_id=1, source_target_pairs={{16,0},{32,16},{48,32},{64,48},{80,64},{96,80},{112,96},{17,1},{33... | collective-permute-start | bytes 786440 | tf_op jit(solution)/shard_map/ppermute | solution.py:23
  112.4 14.0 %collective-permute-start.17 = (f32[2,128,128]{2,1,0:T(8,128)}, f32[2,128,128]{2,1,0:T(8,128)S(1)}, u32[]{:S(2)}, u32[]{:S(2)}) collective-permute-start(f32[2,128,128]{2,1,0:T(8,128)} %collective-permute-done.16), channel_id=1, source_target_pairs={{16,0},{32,16},{48,32},{64,48},{80,64},{96,80},{112,96},{17,1},{33... | collective-permute-start | bytes 393224 | tf_op jit(solution)/shard_map/ppermute | solution.py:31
  117.8 33.8 %collective-permute-start.25 = (f32[2,128,128]{2,1,0:T(8,128)S(1)}, f32[2,128,128]{2,1,0:T(8,128)S(1)}, u32[]{:S(2)}, u32[]{:S(2)}) collective-permute-start(f32[2,128,128]{2,1,0:T(8,128)S(1)} %broadcast_select_fusion.2), channel_id=1, source_target_pairs={{0,16},{16,32},{32,48},{48,64},{64,80},{80,96},{96,112},{1,17},{17... | collective-permute-start | bytes 393224 | tf_op jit(solution)/shard_map/ppermute | solution.py:31
  122.0 7.0 collective-permute-start.18
  125.1 12.9 %collective-permute-start.23 = (f32[2,128,128]{2,1,0:T(8,128)S(1)}, f32[2,128,128]{2,1,0:T(8,128)S(1)}, u32[]{:S(2)}, u32[]{:S(2)}) collective-permute-start(f32[2,128,128]{2,1,0:T(8,128)S(1)} %broadcast_select_fusion.3), channel_id=1, source_target_pairs={{1,0},{2,1},{3,2},{4,3},{5,4},{6,5},{7,6},{8,7},{9,8},{10,9},{11,1... | collective-permute-start | bytes 393224 | tf_op jit(solution)/shard_map/ppermute | solution.py:31
  126.4 15.5 %collective-permute-start.20 = (f32[2,128,128]{2,1,0:T(8,128)}, f32[2,128,128]{2,1,0:T(8,128)S(1)}, u32[]{:S(2)}, u32[]{:S(2)}) collective-permute-start(f32[2,128,128]{2,1,0:T(8,128)} %collective-permute-done.19), channel_id=1, source_target_pairs={{16,0},{32,16},{48,32},{64,48},{80,64},{96,80},{112,96},{17,1},{33... | collective-permute-start | bytes 393224 | tf_op jit(solution)/shard_map/ppermute | solution.py:31
  129.0 15.7 %collective-permute-start.21 = (f32[2,128,128]{2,1,0:T(8,128)}, f32[2,128,128]{2,1,0:T(8,128)S(1)}, u32[]{:S(2)}, u32[]{:S(2)}) collective-permute-start(f32[2,128,128]{2,1,0:T(8,128)} %broadcast_select_fusion.5), channel_id=1, source_target_pairs={{1,0},{2,1},{3,2},{4,3},{5,4},{6,5},{7,6},{8,7},{9,8},{10,9},{11,1... | collective-permute-start | bytes 393224 | tf_op jit(solution)/shard_map/ppermute | solution.py:31
  131.0 18.1 %collective-permute-start.22 = (f32[2,128,128]{2,1,0:T(8,128)}, f32[2,128,128]{2,1,0:T(8,128)S(1)}, u32[]{:S(2)}, u32[]{:S(2)}) collective-permute-start(f32[2,128,128]{2,1,0:T(8,128)} %broadcast_select_fusion.4), channel_id=1, source_target_pairs={{0,1},{1,2},{2,3},{3,4},{4,5},{5,6},{6,7},{7,8},{8,9},{9,10},{10,1... | collective-permute-start | bytes 393224 | tf_op jit(solution)/shard_map/ppermute | solution.py:31
  138.0 14.3 %collective-permute-start.27 = (f32[2,128,128]{2,1,0:T(8,128)}, f32[2,128,128]{2,1,0:T(8,128)S(1)}, u32[]{:S(2)}, u32[]{:S(2)}) collective-permute-start(f32[2,128,128]{2,1,0:T(8,128)} %collective-permute-done.26), channel_id=1, source_target_pairs={{0,16},{16,32},{32,48},{48,64},{64,80},{80,96},{96,112},{1,17},{17... | collective-permute-start | bytes 393224 | tf_op jit(solution)/shard_map/ppermute | solution.py:31
  141.9 9.1 collective-permute-start.24
  144.7 10.4 collective-permute-start.14
  149.0 11.1 %collective-permute-start.15 = (f32[2,640,64]{1,2,0:T(8,128)S(1)}, f32[2,640,64]{1,2,0:T(8,128)S(1)}, u32[]{:S(2)}, u32[]{:S(2)}) collective-permute-start(f32[2,640,64]{1,2,0:T(8,128)S(1)} %get-tuple-element.725), channel_id=1, source_target_pairs={{1,0},{2,1},{3,2},{4,3},{5,4},{6,5},{7,6},{8,7},{9,8},{10,9},{11,1... | collective-permute-start | bytes 983048 | tf_op jit(solution)/shard_map/ppermute | solution.py:23
  571.6 10.0 collective-permute-start.28
  584.6 137.0 %collective-permute-start.29 = (f32[3,64,640]{2,1,0:T(8,128)S(1)}, f32[3,64,640]{2,1,0:T(8,128)S(1)}, u32[]{:S(2)}, u32[]{:S(2)}) collective-permute-start(f32[3,64,640]{2,1,0:T(8,128)S(1)} %slice.318), channel_id=1, source_target_pairs={{16,0},{32,16},{48,32},{64,48},{80,64},{96,80},{112,96},{17,1},{33... | collective-permute-start | bytes 1474568 | tf_op jit(solution)/shard_map/ppermute | solution.py:31
  725.4 204.4 %collective-permute-start.30 = (f32[3,640,64]{1,2,0:T(8,128)S(1)}, f32[3,640,64]{1,2,0:T(8,128)S(1)}, u32[]{:S(2)}, u32[]{:S(2)}) collective-permute-start(f32[3,640,64]{1,2,0:T(8,128)S(1)} %copy.127), channel_id=1, source_target_pairs={{0,1},{1,2},{2,3},{3,4},{4,5},{5,6},{6,7},{7,8},{8,9},{9,10},{10,1... | collective-permute-start | bytes 1474568 | tf_op jit(solution)/shard_map/ppermute | solution.py:31
  738.5 285.1 %all-reduce.5.cloned.1.call-start = ((), (), s32[]{:S(2)}) async-start(), calls=%async_computation | async-start | bytes 393216 | tf_op jit(solution)/shard_map/psum | solution.py:208
  942.5 83.6 %collective-permute-start.31 = (f32[3,640,64]{1,2,0:T(8,128)S(1)}, f32[3,640,64]{1,2,0:T(8,128)S(1)}, u32[]{:S(2)}, u32[]{:S(2)}) collective-permute-start(f32[3,640,64]{1,2,0:T(8,128)S(1)} %copy.129), channel_id=1, source_target_pairs={{1,0},{2,1},{3,2},{4,3},{5,4},{6,5},{7,6},{8,7},{9,8},{10,9},{11,1... | collective-permute-start | bytes 1474568 | tf_op jit(solution)/shard_map/ppermute | solution.py:31
  (10 other events, 534.6 us)
Sparse Core Ops, SparseCore 0:
  738.6 191.1 all-reduce.6
  933.3 90.2 all-reduce.4
